TPU v7x, 512 devices: a whole 4x4x16 slice. The times are simulated.
512 devices in a mesh: rows: 128 (over y_lo, x, z), cols: 4 (over y_hi, core).
Axes of the slice: x: 4, y: 4 (y_hi: 2, y_lo: 2; y = y_hi * 2 + y_lo), z: 16, core: 2. Of those that a mesh axis runs over, the one named last changes fastest.
Arguments:
- grad_out: bfloat16 [512, 512, 192], P(('rows', 'cols')), may hold values from -6 to 6
- inputs: bfloat16 [1024, 1024, 192], P('rows', 'cols'), may hold values from -6 to 6
- weight: bfloat16 [3, 3, 192, 192], replicated, may hold values from -0.15625 to 0.15625
Outputs:
- input_grad: bfloat16 [1024, 1024, 192], P('rows', 'cols')
- filter_grad: float32 [3, 3, 192, 192], replicated
All inputs are finite; a program needn't handle non-finite values.
Results may differ from a plain program's by a relative error of at most 0.0028.
Values may be sent and summed in bfloat16 or wider, within the bound.
No kernel may reach another device: no remote copies, remote signals or barrier semaphores. Data moves between devices by JAX's collectives and lax.ppermute only.
A program may use at most 64 MiB of HBM per device.

v0:
```python
import functools
import math

import jax
import jax.numpy as jnp
from jax import lax
from jax.experimental import pallas as pl
from jax.experimental.pallas import tpu as pltpu
from jax.sharding import Mesh
from jax.sharding import PartitionSpec as P


AXES = ("r0", "r1", "z1", "z0", "c0", "c1")
ROWS = ("r0", "r1", "z1", "z0")
COLS = ("c0", "c1")
NEAR = ("r0", "r1", "z0", "c0")
FAR = "z1"
CORE = "c1"
BF = jnp.bfloat16
F32 = jnp.float32
LANES = 128
TOTAL = 3072
NT = (((1,), (1,)), ((), ()))
TN = (((0,), (0,)), ((), ()))
STEPS = 32256.0
SMALLEST = 2.0**-126
NN = (((1,), (0,)), ((), ()))


def mm(a, b, dims):
    return lax.dot_general(a, b, dims, preferred_element_type=F32)


def call(body, outs, flops, moved):
    return pl.pallas_call(
        body,
        out_shape=outs,
        cost_estimate=pl.CostEstimate(flops=flops, bytes_accessed=moved, transcendentals=0),
        compiler_params=pltpu.CompilerParams(vmem_limit_bytes=24 * 1024 * 1024),
    )


def split_matrix(width):
    half = width // 2
    q = lax.broadcasted_iota(jnp.int32, (width, width), 0)
    n = lax.broadcasted_iota(jnp.int32, (width, width), 1)
    source = jnp.where(n < half, 2 * n, 2 * (n - half) + 1)
    return jnp.where(q == source, 1.0, 0.0).astype(BF)


def send_body(grad_ref, out_ref):
    chans, width = grad_ref.shape
    blocks = out_ref.shape[0]
    block = width // blocks
    r = lax.broadcasted_iota(jnp.int32, (8, width), 0)
    q = lax.broadcasted_iota(jnp.int32, (8, width), 1)
    pick = jnp.where(q == (r + 1) * block, 1.0, 0.0).astype(BF)
    edge = mm(pick, grad_ref[...], NT)
    head = edge[:, :LANES].astype(BF)
    tail = jnp.concatenate([edge[:, LANES:], jnp.zeros((8, 2 * LANES - chans), F32)], axis=1).astype(BF)
    for d in range(blocks):
        out_ref[d, :chans, :] = grad_ref[:, d * block : (d + 1) * block]
        out_ref[d, chans:, :] = jnp.concatenate(
            [head[d : d + 1], tail[d : d + 1], jnp.zeros((6, LANES), BF)], axis=0
        )


def split_body(lines_ref, row_ref, split_ref):
    rows, chans, width = lines_ref.shape
    flat = lines_ref[...].reshape(rows * chans, width)
    flat = mm(flat, split_matrix(width), NN).astype(BF).reshape(rows, chans, width)
    split_ref[...] = flat
    row_ref[...] = flat[rows - 1]


def shifted(grads, edges):
    q = lax.broadcasted_iota(jnp.int32, (LANES, LANES), 0)
    n = lax.broadcasted_iota(jnp.int32, (LANES, LANES), 1)
    move = jnp.where(q == n + 1, 1.0, 0.0).astype(BF)
    r = lax.broadcasted_iota(jnp.int32, (8, LANES), 0)
    lane = lax.broadcasted_iota(jnp.int32, (8, LANES), 1)
    out = []
    for k, block in enumerate(grads):
        place = jnp.where((r == k) & (lane == LANES - 1), 1.0, 0.0).astype(BF)
        out.append((mm(block, move, NN) + mm(edges, place, TN)).astype(BF))
    return out


def edges_of(blocks, chans):
    rows = [jnp.concatenate([b[chans : chans + 1, :], b[chans + 1 : chans + 2, : chans - LANES]], axis=1) for b in blocks]
    rows.append(jnp.zeros((8 - len(rows), chans), BF))
    return jnp.concatenate(rows, axis=0)


def filter_body(got_ref, split_ref, above_ref, out_ref, pair_ref):
    rows, chans, _ = split_ref.shape
    half = rows // 2
    mine = lax.axis_index(CORE)
    blocks = [got_ref[k] for k in range(half)]
    grads = [b[:chans, :] for b in blocks]
    moved = shifted(grads, edges_of(blocks, chans))
    for k in range(half):
        pair_ref[k, 0] = grads[k]
        pair_ref[k, 1] = moved[k]
    spare = jnp.zeros((2 * LANES - chans, half * LANES), BF)
    here = jnp.concatenate([jnp.concatenate(grads, axis=1), spare], axis=0)
    right = jnp.concatenate([jnp.concatenate(moved, axis=1), spare], axis=0)

    def line(p, odd):
        lanes = slice(LANES, 2 * LANES) if odd else slice(0, LANES)
        return above_ref[:, lanes] if p < 0 else split_ref[p, :, lanes]

    own = out_ref.shape[1]

    def put(base, value):
        count = value.shape[0]
        for core in range(2):
            low, high = max(base, core * own), min(base + count, (core + 1) * own)
            if low < high:
                out_ref[mine ^ core, low - core * own : high - core * own, :] = value[low - base : high - base]

    step = chans + chans // 2
    for a in range(3):
        for b in range(3):
            left = jnp.concatenate([line(2 * k + a - 1, b != 1) for k in range(half)], axis=1)
            term = mm(left, right if b == 0 else here, NT)
            base = (3 * a + b) * step
            far = term[:, LANES:]
            put(base, term[:, :LANES])
            put(base + chans, far[: chans // 2] + pltpu.roll(far[chans // 2 :], LANES // 2, 1))
    put(9 * step, jnp.zeros((TOTAL - 9 * step, LANES), F32))


def pair_body(mine_ref, other_ref, out_ref):
    out_ref[...] = (mine_ref[0] + other_ref[...]).astype(BF)


def coded(value, top):
    count = jnp.floor(jnp.abs(value) * (STEPS / top) + 0.5)
    power = jnp.floor(count * (1.0 / 128.0))
    rest = count - 128.0 * power
    code = (1.0 + rest * (1.0 / 128.0)) * SMALLEST
    power = power.astype(jnp.int32)
    for bit in (0, 1, 2, 3, 4, 5, 6, 7, 7):
        code = jnp.where((power & (1 << bit)) != 0, code * 2.0 ** min(1 << bit, 64), code)
    return jnp.where(value < 0, -code, code).astype(BF)


def decoded(code, top):
    code = code.astype(F32)
    size = jnp.abs(code)
    big = size >= 4.0
    power = jnp.where(big, 128.0, 0.0)
    for _ in range(2):
        size = jnp.where(big, size * 2.0**-64, size)
    for bit in range(6, -1, -1):
        span = float(1 << bit)
        big = size >= SMALLEST * 2.0**span
        size = jnp.where(big, size * 2.0**-span, size)
        power = jnp.where(big, power + span, power)
    count = 128.0 * power + (size * (1.0 / SMALLEST) - 1.0) * 128.0
    return jnp.where(code < 0, -count, count) * (top * (1.0 / STEPS))


def near_body(in_ref, out_ref):
    total = jnp.sum(in_ref[...].astype(F32), axis=0)
    chunk = total.shape[0]
    top = jnp.max(jnp.max(jnp.abs(total), axis=0, keepdims=True), axis=1, keepdims=True)
    top = jnp.maximum(top * 1.0078125, 1e-30).astype(BF)
    code = coded(total, top.astype(F32))
    head = jnp.broadcast_to(top, (8, LANES))
    for k in range(out_ref.shape[0]):
        out_ref[k, :chunk, :] = code
        out_ref[k, chunk:, :] = head


def far_body(in_ref, out_ref):
    chunk = out_ref.shape[1]
    total = None
    for k in range(in_ref.shape[0]):
        top = in_ref[k, chunk:, :].astype(F32)[:1]
        term = decoded(in_ref[k, :chunk, :], top)
        total = term if total is None else total + term
    out_ref[...] = jnp.broadcast_to(total.astype(BF)[None], out_ref.shape)


def unpack_body(scale, in_ref, out_ref, whole, sem):
    chans = out_ref.shape[-1]
    step = chans + chans // 2
    copies = []
    for t in range(9):
        base = t * step
        near = in_ref[base : base + chans, :].astype(F32) * scale
        far = in_ref[base + chans : base + step, :].astype(F32) * scale
        whole[t, :, :LANES] = near
        whole[t, : chans // 2, LANES:] = far[:, : LANES // 2]
        whole[t, chans // 2 :, LANES:] = pltpu.roll(far, LANES // 2, 1)[:, : LANES // 2]
        copy = pltpu.make_async_copy(whole.at[t], out_ref.at[t], sem.at[t])
        copy.start()
        copies.append(copy)
    for copy in copies:
        copy.wait()


def input_body(pair_ref, below_ref, weight_ref, out_ref):
    rows, _, width = out_ref.shape
    half = rows // 2
    grads = [pair_ref[k, 0] for k in range(half)] + [below_ref[0]]
    moved = [pair_ref[k, 1] for k in range(half)] + [below_ref[1]]
    here = jnp.concatenate(grads[:half], axis=1)
    right = jnp.concatenate(moved[:half], axis=1)
    here_down = jnp.concatenate(grads[1:], axis=1)
    right_down = jnp.concatenate(moved[1:], axis=1)

    def tap(a, b, g):
        return mm(weight_ref[a, b], g, NN)

    even_even = tap(1, 1, here)
    even_odd = tap(1, 2, here) + tap(1, 0, right)
    odd_even = tap(2, 1, here) + tap(0, 1, here_down)
    odd_odd = tap(2, 2, here) + tap(2, 0, right) + tap(0, 2, here_down) + tap(0, 0, right_down)
    q = lax.broadcasted_iota(jnp.int32, (width, width), 1)
    n = lax.broadcasted_iota(jnp.int32, (width, width), 0)
    target = jnp.where(n < LANES, 2 * n, 2 * (n - LANES) + 1)
    merge = jnp.where(q == target, 1.0, 0.0).astype(BF)
    for k in range(half):
        cut = slice(k * LANES, (k + 1) * LANES)
        for p, left, odd in ((2 * k, even_even, even_odd), (2 * k + 1, odd_even, odd_odd)):
            both = jnp.concatenate([left[:, cut], odd[:, cut]], axis=1).astype(BF)
            out_ref[p] = mm(both, merge, NN).astype(BF)


def shape(dims, dtype):
    return jax.ShapeDtypeStruct(dims, dtype)


def moved_rows(x, by):
    devices = lax.axis_size(ROWS)
    pairs = [(i, i + by) for i in range(devices) if 0 <= i + by < devices]
    return lax.ppermute(x, ROWS, pairs)


def swap(x, axes):
    return lax.all_to_all(x, axes, split_axis=0, concat_axis=0, tiled=True)


def step(grad_out, inputs, weight):
    chans = weight.shape[2]
    rows, cols = inputs.shape[:2]
    half = rows // 2
    near, far = lax.axis_size(NEAR), lax.axis_size(FAR)
    own = TOTAL // lax.axis_size(CORE)
    chunk = own // near
    positions = half * lax.axis_size(ROWS) * (cols // 2) * lax.axis_size(COLS)
    grad = jnp.transpose(grad_out, (0, 2, 1))[0]
    lines = jnp.transpose(inputs, (0, 2, 1))

    sent = call(send_body, shape((lax.axis_size(COLS), chans + 8, LANES), BF), 10**8, 5 * 10**5)(grad)
    got = swap(sent, COLS)
    last, split = call(
        split_body, (shape((chans, cols), BF), shape((rows, chans, cols), BF)), 2 * 10**8, 2 * 10**6
    )(lines)
    above = moved_rows(last, 1)
    terms, pairs = call(
        filter_body,
        (shape((2, own, LANES), F32), shape((half, 2, chans, LANES), BF)),
        10**9,
        4 * 10**6,
    )(got, split, above)
    other = lax.ppermute(terms[1], CORE, [(0, 1), (1, 0)])
    part = call(pair_body, shape((own, LANES), BF), 10**6, 2 * 10**6)(terms, other)
    part, pairs = lax.optimization_barrier((part, pairs))
    below = moved_rows(pairs[0], -1)
    part = swap(part.reshape(near, chunk, LANES), NEAR)
    part = call(near_body, shape((far, chunk + 8, LANES), BF), 10**6, 10**6)(part)
    part, pairs = lax.optimization_barrier((part, pairs))
    part = swap(part, FAR)
    input_grad = call(input_body, shape((rows, chans, cols), BF), 10**9, 2 * 10**6)(pairs, below, weight)
    part, input_grad = lax.optimization_barrier((part, input_grad))
    part = call(far_body, shape((near, chunk, LANES), BF), 10**6, 10**6)(part)
    part = swap(part, NEAR).reshape(own, LANES)
    whole = lax.all_gather(part, CORE, axis=0, tiled=True)
    filter_grad = pl.pallas_call(
        functools.partial(unpack_body, 1.0 / math.sqrt(positions)),
        out_shape=shape((9, chans, chans), F32),
        out_specs=pl.BlockSpec(memory_space=pltpu.HBM),
        scratch_shapes=[pltpu.VMEM((9, chans, chans), F32), pltpu.SemaphoreType.DMA((9,))],
        cost_estimate=pl.CostEstimate(flops=10**6, bytes_accessed=2 * 10**6, transcendentals=0),
        compiler_params=pltpu.CompilerParams(vmem_limit_bytes=24 * 1024 * 1024),
    )(whole)
    return (jnp.transpose(input_grad, (0, 2, 1)), filter_grad.reshape(3, 3, chans, chans))


def solution(mesh):
    split = Mesh(mesh.devices.reshape(2, 4, 8, 2, 2, 2), AXES)
    return build(split)


def build(split):
    return jax.shard_map(
        step,
        mesh=split,
        in_specs=(P(ROWS + COLS, None, None), P(ROWS, COLS, None), P()),
        out_specs=(P(ROWS, COLS, None), P()),
        check_vma=False,
    )
```

profile of v0, /device:TPU:1, one launch (start us, length us, event | category | flops | bytes accessed | tf_op | source)
XLA Modules:
  0.0 90.3 jit_solution(10455233349901398443)
XLA Ops:
  0.6 0.0 copy-start.1
  0.6 0.9 %copy-done.1 = bf16[1,512,192]{1,2,0:T(8,128)(2,1)S(1)} copy-done((bf16[1,512,192]{1,2,0:T(8,128)(2,1)S(1)}, bf16[1,512,192]{1,2,0:T(8,128)(2,1)}, u32[]{:S(2)}) %copy-start.1) | copy-done | bytes 196632
  1.6 0.9 shard_map.50
  2.4 10.2 %all-to-all-start = ((bf16[4,200,128]{2,1,0:T(8,128)(2,1)}), bf16[4,200,128]{2,1,0:T(8,128)(2,1)S(1)}, u32[]{:S(2)}, u32[]{:S(2)}) async-start(bf16[4,200,128]{2,1,0:T(8,128)(2,1)} %shard_map.50), calls=%async_computation | async-start | bytes 409600 | tf_op jit(solution)/shard_map/all_to_all | solution.py:244
  12.6 0.0 copy-start
  12.6 1.1 %copy-done = bf16[8,256,192]{1,2,0:T(8,128)(2,1)S(1)} copy-done((bf16[8,256,192]{1,2,0:T(8,128)(2,1)S(1)}, bf16[8,256,192]{1,2,0:T(8,128)(2,1)}, u32[]{:S(2)}) %copy-start) | copy-done | bytes 786456
  13.7 0.4 shard_map.51
  14.1 1.3 %collective-permute-start = (bf16[192,256]{1,0:T(8,128)(2,1)S(1)}, bf16[192,256]{1,0:T(8,128)(2,1)S(1)}, u32[]{:S(2)}, u32[]{:S(2)}) collective-permute-start(bf16[192,256]{1,0:T(8,128)(2,1)S(1)} %get-tuple-element.13), channel_id=1, source_target_pairs={{0,4},{4,8},{8,12},{12,16},{16,20},{20,24},{24,28},{28,32},{32,36}... | collective-permute-start | bytes 294920 | tf_op jit(solution)/shard_map/ppermute | solution.py:240
  15.4 2.4 %collective-permute-done.above_ref = bf16[192,256]{1,0:T(8,128)(2,1)S(1)} collective-permute-done((bf16[192,256]{1,0:T(8,128)(2,1)S(1)}, bf16[192,256]{1,0:T(8,128)(2,1)S(1)}, u32[]{:S(2)}, u32[]{:S(2)}) %collective-permute-start) | collective-permute-done | bytes 98336 | tf_op jit(solution)/shard_map/ppermute | solution.py:240
  17.8 0.5 all-to-all-done.got_ref
  18.2 1.0 %shard_map.52 = (f32[2,1536,128]{2,1,0:T(8,128)S(1)}, bf16[4,2,192,128]{3,2,1,0:T(8,128)(2,1)S(1)}) custom-call(bf16[4,200,128]{2,1,0:T(8,128)(2,1)S(1)} %all-to-all-done.got_ref, bf16[8,192,256]{2,1,0:T(8,128)(2,1)S(1)} %get-tuple-element.12.split_ref, bf16[192,256]{1,0:T(8,128)(2,1)S(1)} %collective-permute-done.above_ref), custom_call_target="tpu_custom_call" | custom-call | flops 1000000000 | bytes 4000000 | tf_op jit(solution)/shard_map/pallas_call | solution.py:264
  19.2 0.1 slice_bitcast_fusion
  19.3 0.0 copy-start.2
  19.3 3.3 %collective-permute-start.1 = (f32[1536,128]{1,0:T(8,128)S(1)}, f32[1536,128]{1,0:T(8,128)S(1)}, u32[]{:S(2)}, u32[]{:S(2)}) collective-permute-start(f32[1536,128]{1,0:T(8,128)S(1)} %slice_bitcast_fusion), channel_id=1, source_target_pairs={{0,1},{1,0},{2,3},{3,2},{4,5},{5,4},{6,7},{7,6},{8,9},{9,8},{10,11... | collective-permute-start | bytes 2359304 | tf_op jit(solution)/shard_map/ppermute | solution.py:270
  22.6 1.9 %collective-permute-done.1.other_ref = f32[1536,128]{1,0:T(8,128)S(1)} collective-permute-done((f32[1536,128]{1,0:T(8,128)S(1)}, f32[1536,128]{1,0:T(8,128)S(1)}, u32[]{:S(2)}, u32[]{:S(2)}) %collective-permute-start.1) | collective-permute-done | bytes 786464 | tf_op jit(solution)/shard_map/ppermute | solution.py:270
  24.5 0.1 shard_map.53
  24.6 22.3 %all_to_all.20.in_ref = bf16[32,48,128]{2,1,0:T(8,128)(2,1)S(1)} all-to-all(bf16[32,48,128]{2,1,0:T(8,128)(2,1)S(1)} %bitcast.12), channel_id=1, replica_groups=mesh['r0'=2,'r1'=4,'z1'=8,'z0'=2,'c0'=2,'c1'=2] {'r0','r1','z0','c0'}, dimensions={0} | all-to-all | bytes 786432 | tf_op jit(solution)/shard_map/all_to_all | solution.py:244
  46.9 0.9 shard_map.54
  47.7 8.3 %all-to-all-start.2 = ((bf16[8,56,128]{2,1,0:T(8,128)(2,1)}), bf16[8,56,128]{2,1,0:T(8,128)(2,1)S(1)}, u32[]{:S(2)}, u32[]{:S(2)}) async-start(bf16[8,56,128]{2,1,0:T(8,128)(2,1)} %shard_map.54), calls=%async_computation.2 | async-start | bytes 229376 | tf_op jit(solution)/shard_map/all_to_all | solution.py:244
  56.0 1.3 %collective-permute-start.2 = (bf16[2,192,128]{2,1,0:T(8,128)(2,1)S(1)}, bf16[2,192,128]{2,1,0:T(8,128)(2,1)S(1)}, u32[]{:S(2)}, u32[]{:S(2)}) collective-permute-start(bf16[2,192,128]{2,1,0:T(8,128)(2,1)S(1)} %slice_bitcast_fusion.1), channel_id=1, source_target_pairs={{4,0},{8,4},{12,8},{16,12},{20,16},{24,20},{28,24},{32,28},{36,32}... | collective-permute-start | bytes 294920 | tf_op jit(solution)/shard_map/ppermute | solution.py:240
  57.3 4.7 %collective-permute-done.2.below_ref = bf16[2,192,128]{2,1,0:T(8,128)(2,1)S(1)} collective-permute-done((bf16[2,192,128]{2,1,0:T(8,128)(2,1)S(1)}, bf16[2,192,128]{2,1,0:T(8,128)(2,1)S(1)}, u32[]{:S(2)}, u32[]{:S(2)}) %collective-permute-start.2) | collective-permute-done | bytes 98336 | tf_op jit(solution)/shard_map/ppermute | solution.py:240
  62.0 0.0 copy-done.2
  62.0 1.8 %shard_map.55 = bf16[8,192,256]{2,1,0:T(8,128)(2,1)} custom-call(bf16[4,2,192,128]{3,2,1,0:T(8,128)(2,1)S(1)} %get-tuple-element.19.pair_ref, bf16[2,192,128]{2,1,0:T(8,128)(2,1)S(1)} %collective-permute-done.2.below_ref, bf16[3,3,192,192]{3,2,1,0:T(8,128)(2,1)S(1)} %copy-done.2), custom_call_target="tpu_custom_call" | custom-call | flops 1000000000 | bytes 2000000 | tf_op jit(solution)/shard_map/pallas_call | solution.py:278
  63.7 4.8 %all-to-all-done.2.in_ref = bf16[8,56,128]{2,1,0:T(8,128)(2,1)S(1)} async-done(((bf16[8,56,128]{2,1,0:T(8,128)(2,1)}), bf16[8,56,128]{2,1,0:T(8,128)(2,1)S(1)}, u32[]{:S(2)}, u32[]{:S(2)}) %all-to-all-start.2) | async-done | bytes 114720 | tf_op jit(solution)/shard_map/all_to_all | solution.py:244
  68.5 0.4 shard_map.56
  68.9 12.5 %all_to_all.21 = bf16[32,48,128]{2,1,0:T(8,128)(2,1)S(1)} all-to-all(bf16[32,48,128]{2,1,0:T(8,128)(2,1)S(1)} %shard_map.56), channel_id=1, replica_groups=mesh['r0'=2,'r1'=4,'z1'=8,'z0'=2,'c0'=2,'c1'=2] {'r0','r1','z0','c0'}, dimensions={0} | all-to-all | bytes 786432 | tf_op jit(solution)/shard_map/all_to_all | solution.py:244
  81.4 7.6 %all_gather.3.in_ref = bf16[3072,128]{1,0:T(8,128)(2,1)S(1)} all-gather(bf16[1536,128]{1,0:T(8,128)(2,1)S(1)} %bitcast.16), channel_id=1, replica_groups=mesh['r0'=2,'r1'=4,'z1'=8,'z0'=2,'c0'=2,'c1'=2] {'c1'}, dimensions={0}, use_global_device_ids=true | all-gather | bytes 1179648 | tf_op jit(solution)/shard_map/all_gather | solution.py:282
  89.0 1.4 %shard_map.57 = f32[9,192,192]{2,1,0:T(8,128)} custom-call(bf16[3072,128]{1,0:T(8,128)(2,1)S(1)} %all_gather.3.in_ref), custom_call_target="tpu_custom_call" | custom-call | flops 1000000 | bytes 2000000 | tf_op jit(solution)/shard_map/pallas_call | solution.py:283
  (1 shorter events, 0.0 us)
Async XLA Ops:
  0.6 0.9 %copy-start.1 = (bf16[1,512,192]{1,2,0:T(8,128)(2,1)S(1)}, bf16[1,512,192]{1,2,0:T(8,128)(2,1)}, u32[]{:S(2)}) copy-start(bf16[1,512,192]{1,2,0:T(8,128)(2,1)} %param.3) | copy-start | bytes 589828
  2.4 15.8 %all-to-all-start = ((bf16[4,200,128]{2,1,0:T(8,128)(2,1)}), bf16[4,200,128]{2,1,0:T(8,128)(2,1)S(1)}, u32[]{:S(2)}, u32[]{:S(2)}) async-start(bf16[4,200,128]{2,1,0:T(8,128)(2,1)} %shard_map.50), calls=%async_computation | async-start | bytes 409600 | tf_op jit(solution)/shard_map/all_to_all | solution.py:244
  12.6 1.1 %copy-start = (bf16[8,256,192]{1,2,0:T(8,128)(2,1)S(1)}, bf16[8,256,192]{1,2,0:T(8,128)(2,1)}, u32[]{:S(2)}) copy-start(bf16[8,256,192]{1,2,0:T(8,128)(2,1)} %param.4) | copy-start | bytes 2359300
  14.1 3.7 %collective-permute-start = (bf16[192,256]{1,0:T(8,128)(2,1)S(1)}, bf16[192,256]{1,0:T(8,128)(2,1)S(1)}, u32[]{:S(2)}, u32[]{:S(2)}) collective-permute-start(bf16[192,256]{1,0:T(8,128)(2,1)S(1)} %get-tuple-element.13), channel_id=1, source_target_pairs={{0,4},{4,8},{8,12},{12,16},{16,20},{20,24},{24,28},{28,32},{32,36}... | collective-permute-start | bytes 294920 | tf_op jit(solution)/shard_map/ppermute | solution.py:240
  19.3 42.7 %copy-start.2 = (bf16[3,3,192,192]{3,2,1,0:T(8,128)(2,1)S(1)}, bf16[3,3,192,192]{3,2,1,0:T(8,128)(2,1)}, u32[]{:S(2)}) copy-start(bf16[3,3,192,192]{3,2,1,0:T(8,128)(2,1)} %weight_ref.1) | copy-start | bytes 1990660
  19.3 5.2 %collective-permute-start.1 = (f32[1536,128]{1,0:T(8,128)S(1)}, f32[1536,128]{1,0:T(8,128)S(1)}, u32[]{:S(2)}, u32[]{:S(2)}) collective-permute-start(f32[1536,128]{1,0:T(8,128)S(1)} %slice_bitcast_fusion), channel_id=1, source_target_pairs={{0,1},{1,0},{2,3},{3,2},{4,5},{5,4},{6,7},{7,6},{8,9},{9,8},{10,11... | collective-permute-start | bytes 2359304 | tf_op jit(solution)/shard_map/ppermute | solution.py:270
  47.7 20.8 %all-to-all-start.2 = ((bf16[8,56,128]{2,1,0:T(8,128)(2,1)}), bf16[8,56,128]{2,1,0:T(8,128)(2,1)S(1)}, u32[]{:S(2)}, u32[]{:S(2)}) async-start(bf16[8,56,128]{2,1,0:T(8,128)(2,1)} %shard_map.54), calls=%async_computation.2 | async-start | bytes 229376 | tf_op jit(solution)/shard_map/all_to_all | solution.py:244
  56.0 6.0 %collective-permute-start.2 = (bf16[2,192,128]{2,1,0:T(8,128)(2,1)S(1)}, bf16[2,192,128]{2,1,0:T(8,128)(2,1)S(1)}, u32[]{:S(2)}, u32[]{:S(2)}) collective-permute-start(bf16[2,192,128]{2,1,0:T(8,128)(2,1)S(1)} %slice_bitcast_fusion.1), channel_id=1, source_target_pairs={{4,0},{8,4},{12,8},{16,12},{20,16},{24,20},{28,24},{32,28},{36,32}... | collective-permute-start | bytes 294920 | tf_op jit(solution)/shard_map/ppermute | solution.py:240
where the time goes:
time: 90.8 us; the launch traced here: 90.3 us
  blocking collectives  42.3 us (47%)
  starting transfers between devices  24.3 us (27%)
  waiting for transfers between devices  14.2 us (16%)
  Pallas kernels  6.65 us (7%)
  local copies, waits for them, and re-layouts  2.12 us (2%)
    all_to_all x2, blocking collectives, swap(): return lax.all_to_all(x, axes, split_axis=0, concat_axis=0, tiled=True)  34.7 us
    all_to_all x2, starting transfers between devices, swap(): return lax.all_to_all(x, axes, split_axis=0, concat_axis=0, tiled=True)  18.4 us
    all_gather x1, blocking collectives, step(): whole = lax.all_gather(part, CORE, axis=0, tiled=True)  7.61 us
    ppermute x2, waiting for transfers between devices, moved_rows(): return lax.ppermute(x, ROWS, pairs)  7.04 us
    all_to_all x2, waiting for transfers between devices, swap(): return lax.all_to_all(x, axes, split_axis=0, concat_axis=0, tiled=True)  5.28 us
    ppermute x1, starting transfers between devices, step(): other = lax.ppermute(terms[1], CORE, [(0, 1), (1, 0)])  3.28 us
    ppermute x2, starting transfers between devices, moved_rows(): return lax.ppermute(x, ROWS, pairs)  2.59 us
    unnamed x6, local copies, waits for them, and re-layouts  2.06 us
  transfers between devices with their start and end apart: 5, of which 5 were waited for; matrix products, arithmetic and copies ran while one was open for 0% of the time, Pallas kernels for 2%

commit v1 on v0

--- a/solution.py
+++ b/solution.py
@@ -65,12 +65,10 @@
         )
 
 
-def split_body(lines_ref, row_ref, split_ref):
+def split_body(lines_ref, split_ref):
     rows, chans, width = lines_ref.shape
     flat = lines_ref[...].reshape(rows * chans, width)
-    flat = mm(flat, split_matrix(width), NN).astype(BF).reshape(rows, chans, width)
-    split_ref[...] = flat
-    row_ref[...] = flat[rows - 1]
+    split_ref[...] = mm(flat, split_matrix(width), NN).astype(BF).reshape(rows, chans, width)
 
 
 def shifted(grads, edges):
@@ -93,9 +91,10 @@
 
 
 def filter_body(got_ref, split_ref, above_ref, out_ref, pair_ref):
-    rows, chans, _ = split_ref.shape
+    rows, chans, width = split_ref.shape
     half = rows // 2
     mine = lax.axis_index(CORE)
+    top = mm(above_ref[...], split_matrix(width), NN).astype(BF)
     blocks = [got_ref[k] for k in range(half)]
     grads = [b[:chans, :] for b in blocks]
     moved = shifted(grads, edges_of(blocks, chans))
@@ -108,7 +107,7 @@
 
     def line(p, odd):
         lanes = slice(LANES, 2 * LANES) if odd else slice(0, LANES)
-        return above_ref[:, lanes] if p < 0 else split_ref[p, :, lanes]
+        return top[:, lanes] if p < 0 else split_ref[p, :, lanes]
 
     own = out_ref.shape[1]
 
@@ -257,10 +256,8 @@
 
     sent = call(send_body, shape((lax.axis_size(COLS), chans + 8, LANES), BF), 10**8, 5 * 10**5)(grad)
     got = swap(sent, COLS)
-    last, split = call(
-        split_body, (shape((chans, cols), BF), shape((rows, chans, cols), BF)), 2 * 10**8, 2 * 10**6
-    )(lines)
-    above = moved_rows(last, 1)
+    above = moved_rows(lines[rows - 1], 1)
+    split = call(split_body, shape((rows, chans, cols), BF), 2 * 10**8, 2 * 10**6)(lines)
     terms, pairs = call(
         filter_body,
         (shape((2, own, LANES), F32), shape((half, 2, chans, LANES), BF)),
@@ -268,9 +265,8 @@
         4 * 10**6,
     )(got, split, above)
     other = lax.ppermute(terms[1], CORE, [(0, 1), (1, 0)])
+    below = moved_rows(pairs[0], -1)
     part = call(pair_body, shape((own, LANES), BF), 10**6, 2 * 10**6)(terms, other)
-    part, pairs = lax.optimization_barrier((part, pairs))
-    below = moved_rows(pairs[0], -1)
     part = swap(part.reshape(near, chunk, LANES), NEAR)
     part = call(near_body, shape((far, chunk + 8, LANES), BF), 10**6, 10**6)(part)
     part, pairs = lax.optimization_barrier((part, pairs))

time: 90.8 us -> 90.2 us (level)
    ppermute x2, waiting for transfers between devices: 7.04 us -> 5.53 us  [moved_rows(): return lax.ppermute(x, ROWS, pairs)]
  transfers between devices with their start and end apart: 5 -> 5, of which waited for: 5 -> 5; matrix products, arithmetic and copies ran while one was open for 0% -> 1% of each run, Pallas kernels for 2% -> 2%
where the time goes in v1:
time: 90.2 us; the launch traced here: 89.7 us
  blocking collectives  41.7 us (46%)
  starting transfers between devices  24.3 us (27%)
  waiting for transfers between devices  13.3 us (15%)
  Pallas kernels  6.65 us (7%)
  local copies, waits for them, and re-layouts  3.01 us (3%)
    all_to_all x2, blocking collectives, swap(): return lax.all_to_all(x, axes, split_axis=0, concat_axis=0, tiled=True)  34.1 us
    all_to_all x2, starting transfers between devices, swap(): return lax.all_to_all(x, axes, split_axis=0, concat_axis=0, tiled=True)  18.4 us
    all_gather x1, blocking collectives, step(): whole = lax.all_gather(part, CORE, axis=0, tiled=True)  7.61 us
    all_to_all x2, waiting for transfers between devices, swap(): return lax.all_to_all(x, axes, split_axis=0, concat_axis=0, tiled=True)  5.89 us
    ppermute x2, waiting for transfers between devices, moved_rows(): return lax.ppermute(x, ROWS, pairs)  5.53 us
    ppermute x1, starting transfers between devices, step(): other = lax.ppermute(terms[1], CORE, [(0, 1), (1, 0)])  3.28 us
    ppermute x2, starting transfers between devices, moved_rows(): return lax.ppermute(x, ROWS, pairs)  2.58 us
    unnamed x6, local copies, waits for them, and re-layouts  2.05 us
  transfers between devices with their start and end apart: 5, of which 5 were waited for; matrix products, arithmetic and copies ran while one was open for 1% of the time, Pallas kernels for 2%

profile of v1, /device:TPU:1, one launch (start us, length us, event | category | flops | bytes accessed | tf_op | source)
XLA Modules:
  0.0 89.7 jit_solution(5858974388941052336)
XLA Ops:
  0.6 0.0 copy-start.1
  0.6 0.9 %copy-done.1 = bf16[1,512,192]{1,2,0:T(8,128)(2,1)S(1)} copy-done((bf16[1,512,192]{1,2,0:T(8,128)(2,1)S(1)}, bf16[1,512,192]{1,2,0:T(8,128)(2,1)}, u32[]{:S(2)}) %copy-start.1) | copy-done | bytes 196632
  1.6 0.9 shard_map.50
  2.4 10.2 %all-to-all-start = ((bf16[4,200,128]{2,1,0:T(8,128)(2,1)}), bf16[4,200,128]{2,1,0:T(8,128)(2,1)S(1)}, u32[]{:S(2)}, u32[]{:S(2)}) async-start(bf16[4,200,128]{2,1,0:T(8,128)(2,1)} %shard_map.50), calls=%async_computation | async-start | bytes 409600 | tf_op jit(solution)/shard_map/all_to_all | solution.py:243
  12.6 0.9 %slice_bitcast_fusion.1 = bf16[192,256]{1,0:T(8,128)(2,1)S(1)} fusion(bf16[8,192,256]{2,1,0:T(8,128)(2,1)} %bitcast.15), kind=kLoop, calls=%fused_computation.1 | loop fusion | bytes 196608 | tf_op jit(solution)/shard_map/squeeze | solution.py:259
  13.5 1.3 %collective-permute-start = (bf16[192,256]{1,0:T(8,128)(2,1)S(1)}, bf16[192,256]{1,0:T(8,128)(2,1)S(1)}, u32[]{:S(2)}, u32[]{:S(2)}) collective-permute-start(bf16[192,256]{1,0:T(8,128)(2,1)S(1)} %slice_bitcast_fusion.1), channel_id=1, source_target_pairs={{0,4},{4,8},{8,12},{12,16},{16,20},{20,24},{24,28},{28,32},{32,36}... | collective-permute-start | bytes 294920 | tf_op jit(solution)/shard_map/ppermute | solution.py:239
  14.8 0.0 copy-start
  14.8 1.1 %copy-done = bf16[8,256,192]{1,2,0:T(8,128)(2,1)S(1)} copy-done((bf16[8,256,192]{1,2,0:T(8,128)(2,1)S(1)}, bf16[8,256,192]{1,2,0:T(8,128)(2,1)}, u32[]{:S(2)}) %copy-start) | copy-done | bytes 786456
  15.9 0.4 shard_map.51.split_ref
  16.3 0.9 collective-permute-done.above_ref
  17.1 1.1 %all-to-all-done.got_ref = bf16[4,200,128]{2,1,0:T(8,128)(2,1)S(1)} async-done(((bf16[4,200,128]{2,1,0:T(8,128)(2,1)}), bf16[4,200,128]{2,1,0:T(8,128)(2,1)S(1)}, u32[]{:S(2)}, u32[]{:S(2)}) %all-to-all-start) | async-done | bytes 204832 | tf_op jit(solution)/shard_map/all_to_all | solution.py:243
  18.2 1.0 %shard_map.52 = (f32[2,1536,128]{2,1,0:T(8,128)S(1)}, bf16[4,2,192,128]{3,2,1,0:T(8,128)(2,1)S(1)}) custom-call(bf16[4,200,128]{2,1,0:T(8,128)(2,1)S(1)} %all-to-all-done.got_ref, bf16[8,192,256]{2,1,0:T(8,128)(2,1)S(1)} %shard_map.51.split_ref, bf16[192,256]{1,0:T(8,128)(2,1)S(1)} %collective-permute-done.above_ref), custom_call_target="tpu_custom_call" | custom-call | flops 1000000000 | bytes 4000000 | tf_op jit(solution)/shard_map/pallas_call | solution.py:261
  19.2 0.1 slice_bitcast_fusion
  19.3 0.0 copy-start.2
  19.3 3.3 %collective-permute-start.1 = (f32[1536,128]{1,0:T(8,128)S(1)}, f32[1536,128]{1,0:T(8,128)S(1)}, u32[]{:S(2)}, u32[]{:S(2)}) collective-permute-start(f32[1536,128]{1,0:T(8,128)S(1)} %slice_bitcast_fusion), channel_id=1, source_target_pairs={{0,1},{1,0},{2,3},{3,2},{4,5},{5,4},{6,7},{7,6},{8,9},{9,8},{10,11... | collective-permute-start | bytes 2359304 | tf_op jit(solution)/shard_map/ppermute | solution.py:267
  22.6 1.9 %collective-permute-done.1.other_ref = f32[1536,128]{1,0:T(8,128)S(1)} collective-permute-done((f32[1536,128]{1,0:T(8,128)S(1)}, f32[1536,128]{1,0:T(8,128)S(1)}, u32[]{:S(2)}, u32[]{:S(2)}) %collective-permute-start.1) | collective-permute-done | bytes 786464 | tf_op jit(solution)/shard_map/ppermute | solution.py:267
  24.5 0.1 shard_map.53
  24.6 21.6 %all_to_all.20.in_ref = bf16[32,48,128]{2,1,0:T(8,128)(2,1)S(1)} all-to-all(bf16[32,48,128]{2,1,0:T(8,128)(2,1)S(1)} %bitcast.14), channel_id=1, replica_groups=mesh['r0'=2,'r1'=4,'z1'=8,'z0'=2,'c0'=2,'c1'=2] {'r0','r1','z0','c0'}, dimensions={0} | all-to-all | bytes 786432 | tf_op jit(solution)/shard_map/all_to_all | solution.py:243
  46.2 0.9 shard_map.54
  47.1 8.3 %all-to-all-start.2 = ((bf16[8,56,128]{2,1,0:T(8,128)(2,1)}), bf16[8,56,128]{2,1,0:T(8,128)(2,1)S(1)}, u32[]{:S(2)}, u32[]{:S(2)}) async-start(bf16[8,56,128]{2,1,0:T(8,128)(2,1)} %shard_map.54), calls=%async_computation.2 | async-start | bytes 229376 | tf_op jit(solution)/shard_map/all_to_all | solution.py:243
  55.4 1.3 %collective-permute-start.2 = (bf16[2,192,128]{2,1,0:T(8,128)(2,1)S(1)}, bf16[2,192,128]{2,1,0:T(8,128)(2,1)S(1)}, u32[]{:S(2)}, u32[]{:S(2)}) collective-permute-start(bf16[2,192,128]{2,1,0:T(8,128)(2,1)S(1)} %slice_bitcast_fusion.2), channel_id=1, source_target_pairs={{4,0},{8,4},{12,8},{16,12},{20,16},{24,20},{28,24},{32,28},{36,32}... | collective-permute-start | bytes 294920 | tf_op jit(solution)/shard_map/ppermute | solution.py:239
  56.7 4.7 %collective-permute-done.2.below_ref = bf16[2,192,128]{2,1,0:T(8,128)(2,1)S(1)} collective-permute-done((bf16[2,192,128]{2,1,0:T(8,128)(2,1)S(1)}, bf16[2,192,128]{2,1,0:T(8,128)(2,1)S(1)}, u32[]{:S(2)}, u32[]{:S(2)}) %collective-permute-start.2) | collective-permute-done | bytes 98336 | tf_op jit(solution)/shard_map/ppermute | solution.py:239
  61.3 0.0 copy-done.2
  61.3 1.8 %shard_map.55 = bf16[8,192,256]{2,1,0:T(8,128)(2,1)} custom-call(bf16[4,2,192,128]{3,2,1,0:T(8,128)(2,1)S(1)} %get-tuple-element.11.pair_ref, bf16[2,192,128]{2,1,0:T(8,128)(2,1)S(1)} %collective-permute-done.2.below_ref, bf16[3,3,192,192]{3,2,1,0:T(8,128)(2,1)S(1)} %copy-done.2), custom_call_target="tpu_custom_call" | custom-call | flops 1000000000 | bytes 2000000 | tf_op jit(solution)/shard_map/pallas_call | solution.py:274
  63.1 4.8 %all-to-all-done.2.in_ref = bf16[8,56,128]{2,1,0:T(8,128)(2,1)S(1)} async-done(((bf16[8,56,128]{2,1,0:T(8,128)(2,1)}), bf16[8,56,128]{2,1,0:T(8,128)(2,1)S(1)}, u32[]{:S(2)}, u32[]{:S(2)}) %all-to-all-start.2) | async-done | bytes 114720 | tf_op jit(solution)/shard_map/all_to_all | solution.py:243
  67.9 0.4 shard_map.56
  68.3 12.5 %all_to_all.21 = bf16[32,48,128]{2,1,0:T(8,128)(2,1)S(1)} all-to-all(bf16[32,48,128]{2,1,0:T(8,128)(2,1)S(1)} %shard_map.56), channel_id=1, replica_groups=mesh['r0'=2,'r1'=4,'z1'=8,'z0'=2,'c0'=2,'c1'=2] {'r0','r1','z0','c0'}, dimensions={0} | all-to-all | bytes 786432 | tf_op jit(solution)/shard_map/all_to_all | solution.py:243
  80.7 7.6 %all_gather.3.in_ref = bf16[3072,128]{1,0:T(8,128)(2,1)S(1)} all-gather(bf16[1536,128]{1,0:T(8,128)(2,1)S(1)} %bitcast.19), channel_id=1, replica_groups=mesh['r0'=2,'r1'=4,'z1'=8,'z0'=2,'c0'=2,'c1'=2] {'c1'}, dimensions={0}, use_global_device_ids=true | all-gather | bytes 1179648 | tf_op jit(solution)/shard_map/all_gather | solution.py:278
  88.3 1.4 %shard_map.57 = f32[9,192,192]{2,1,0:T(8,128)} custom-call(bf16[3072,128]{1,0:T(8,128)(2,1)S(1)} %all_gather.3.in_ref), custom_call_target="tpu_custom_call" | custom-call | flops 1000000 | bytes 2000000 | tf_op jit(solution)/shard_map/pallas_call | solution.py:279
  (1 shorter events, 0.0 us)
Async XLA Ops:
  0.6 0.9 %copy-start.1 = (bf16[1,512,192]{1,2,0:T(8,128)(2,1)S(1)}, bf16[1,512,192]{1,2,0:T(8,128)(2,1)}, u32[]{:S(2)}) copy-start(bf16[1,512,192]{1,2,0:T(8,128)(2,1)} %param.3) | copy-start | bytes 589828
  2.4 15.8 %all-to-all-start = ((bf16[4,200,128]{2,1,0:T(8,128)(2,1)}), bf16[4,200,128]{2,1,0:T(8,128)(2,1)S(1)}, u32[]{:S(2)}, u32[]{:S(2)}) async-start(bf16[4,200,128]{2,1,0:T(8,128)(2,1)} %shard_map.50), calls=%async_computation | async-start | bytes 409600 | tf_op jit(solution)/shard_map/all_to_all | solution.py:243
  13.5 3.7 %collective-permute-start = (bf16[192,256]{1,0:T(8,128)(2,1)S(1)}, bf16[192,256]{1,0:T(8,128)(2,1)S(1)}, u32[]{:S(2)}, u32[]{:S(2)}) collective-permute-start(bf16[192,256]{1,0:T(8,128)(2,1)S(1)} %slice_bitcast_fusion.1), channel_id=1, source_target_pairs={{0,4},{4,8},{8,12},{12,16},{16,20},{20,24},{24,28},{28,32},{32,36}... | collective-permute-start | bytes 294920 | tf_op jit(solution)/shard_map/ppermute | solution.py:239
  14.8 1.1 %copy-start = (bf16[8,256,192]{1,2,0:T(8,128)(2,1)S(1)}, bf16[8,256,192]{1,2,0:T(8,128)(2,1)}, u32[]{:S(2)}) copy-start(bf16[8,256,192]{1,2,0:T(8,128)(2,1)} %param.4) | copy-start | bytes 2359300
  19.3 42.1 %copy-start.2 = (bf16[3,3,192,192]{3,2,1,0:T(8,128)(2,1)S(1)}, bf16[3,3,192,192]{3,2,1,0:T(8,128)(2,1)}, u32[]{:S(2)}) copy-start(bf16[3,3,192,192]{3,2,1,0:T(8,128)(2,1)} %weight_ref.1) | copy-start | bytes 1990660
  19.3 5.2 %collective-permute-start.1 = (f32[1536,128]{1,0:T(8,128)S(1)}, f32[1536,128]{1,0:T(8,128)S(1)}, u32[]{:S(2)}, u32[]{:S(2)}) collective-permute-start(f32[1536,128]{1,0:T(8,128)S(1)} %slice_bitcast_fusion), channel_id=1, source_target_pairs={{0,1},{1,0},{2,3},{3,2},{4,5},{5,4},{6,7},{7,6},{8,9},{9,8},{10,11... | collective-permute-start | bytes 2359304 | tf_op jit(solution)/shard_map/ppermute | solution.py:267
  47.1 20.8 %all-to-all-start.2 = ((bf16[8,56,128]{2,1,0:T(8,128)(2,1)}), bf16[8,56,128]{2,1,0:T(8,128)(2,1)S(1)}, u32[]{:S(2)}, u32[]{:S(2)}) async-start(bf16[8,56,128]{2,1,0:T(8,128)(2,1)} %shard_map.54), calls=%async_computation.2 | async-start | bytes 229376 | tf_op jit(solution)/shard_map/all_to_all | solution.py:243
  55.4 6.0 %collective-permute-start.2 = (bf16[2,192,128]{2,1,0:T(8,128)(2,1)S(1)}, bf16[2,192,128]{2,1,0:T(8,128)(2,1)S(1)}, u32[]{:S(2)}, u32[]{:S(2)}) collective-permute-start(bf16[2,192,128]{2,1,0:T(8,128)(2,1)S(1)} %slice_bitcast_fusion.2), channel_id=1, source_target_pairs={{4,0},{8,4},{12,8},{16,12},{20,16},{24,20},{28,24},{32,28},{36,32}... | collective-permute-start | bytes 294920 | tf_op jit(solution)/shard_map/ppermute | solution.py:239

commit v2 on v1

--- a/solution.py
+++ b/solution.py
@@ -48,8 +48,9 @@
     return jnp.where(q == source, 1.0, 0.0).astype(BF)
 
 
-def send_body(grad_ref, out_ref):
+def send_body(grad_ref, line_ref, out_ref, row_ref):
     chans, width = grad_ref.shape
+    row_ref[...] = line_ref[0]
     blocks = out_ref.shape[0]
     block = width // blocks
     r = lax.broadcasted_iota(jnp.int32, (8, width), 0)
@@ -254,9 +255,23 @@
     grad = jnp.transpose(grad_out, (0, 2, 1))[0]
     lines = jnp.transpose(inputs, (0, 2, 1))
 
-    sent = call(send_body, shape((lax.axis_size(COLS), chans + 8, LANES), BF), 10**8, 5 * 10**5)(grad)
+    sent, last = pl.pallas_call(
+        send_body,
+        grid=(1,),
+        in_specs=[
+            pl.BlockSpec(grad.shape, lambda i: (0, 0)),
+            pl.BlockSpec((1, chans, cols), lambda i: (rows - 1, 0, 0)),
+        ],
+        out_specs=[
+            pl.BlockSpec((lax.axis_size(COLS), chans + 8, LANES), lambda i: (0, 0, 0)),
+            pl.BlockSpec((chans, cols), lambda i: (0, 0)),
+        ],
+        out_shape=[shape((lax.axis_size(COLS), chans + 8, LANES), BF), shape((chans, cols), BF)],
+        cost_estimate=pl.CostEstimate(flops=10**8, bytes_accessed=5 * 10**5, transcendentals=0),
+        compiler_params=pltpu.CompilerParams(vmem_limit_bytes=63000000),
+    )(grad, lines)
     got = swap(sent, COLS)
-    above = moved_rows(lines[rows - 1], 1)
+    above = moved_rows(last, 1)
     split = call(split_body, shape((rows, chans, cols), BF), 2 * 10**8, 2 * 10**6)(lines)
     terms, pairs = call(
         filter_body,
@@ -265,16 +280,16 @@
         4 * 10**6,
     )(got, split, above)
     other = lax.ppermute(terms[1], CORE, [(0, 1), (1, 0)])
-    below = moved_rows(pairs[0], -1)
     part = call(pair_body, shape((own, LANES), BF), 10**6, 2 * 10**6)(terms, other)
     part = swap(part.reshape(near, chunk, LANES), NEAR)
     part = call(near_body, shape((far, chunk + 8, LANES), BF), 10**6, 10**6)(part)
     part, pairs = lax.optimization_barrier((part, pairs))
     part = swap(part, FAR)
+    below = moved_rows(pairs[0], -1)
+    part = call(far_body, shape((near, chunk, LANES), BF), 10**6, 10**6)(part)
+    part = swap(part, NEAR).reshape(own, LANES)
     input_grad = call(input_body, shape((rows, chans, cols), BF), 10**9, 2 * 10**6)(pairs, below, weight)
     part, input_grad = lax.optimization_barrier((part, input_grad))
-    part = call(far_body, shape((near, chunk, LANES), BF), 10**6, 10**6)(part)
-    part = swap(part, NEAR).reshape(own, LANES)
     whole = lax.all_gather(part, CORE, axis=0, tiled=True)
     filter_grad = pl.pallas_call(
         functools.partial(unpack_body, 1.0 / math.sqrt(positions)),

time: 90.2 us -> 88.8 us (0.984)
  blocking collectives: 41.7 us -> 48.1 us
  starting transfers between devices: 24.3 us -> 19.8 us
  local copies, waits for them, and re-layouts: 3.01 us -> 0.07 us
  waiting for transfers between devices: 13.3 us -> 11.9 us
  Pallas kernels: 6.65 us -> 7.74 us
    all_to_all x2, blocking collectives: 34.1 us -> 41.7 us  [swap(): return lax.all_to_all(x, axes, split_axis=0, concat_axis=0, tiled=True)]
    all_to_all x2, starting transfers between devices: 18.4 us -> 14.1 us  [swap(): return lax.all_to_all(x, axes, split_axis=0, concat_axis=0, tiled=True)]
    all_to_all x2, waiting for transfers between devices: 5.89 us -> 3.68 us  [swap(): return lax.all_to_all(x, axes, split_axis=0, concat_axis=0, tiled=True)]
    unnamed x6 -> x4, local copies, waits for them, and re-layouts: 2.05 us -> 0.01 us
    all_gather x1, blocking collectives: 7.61 us -> 6.38 us  [step(): whole = lax.all_gather(part, CORE, axis=0, tiled=True)]
    pallas_call x1, Pallas kernels: 0.85 us -> 1.91 us  [step(): pl.pallas_call(send_body, grid=(1,), in_specs=[pl.BlockSpec(grad.shape, l...]
  transfers between devices with their start and end apart: 5 -> 5, of which waited for: 5 -> 5; matrix products, arithmetic and copies ran while one was open for 1% -> 0% of each run, Pallas kernels for 2% -> 2%
where the time goes in v2:
time: 88.8 us; the launch traced here: 88.3 us
  blocking collectives  48.1 us (54%)
  starting transfers between devices  19.8 us (22%)
  waiting for transfers between devices  11.9 us (13%)
  Pallas kernels  7.74 us (9%)
    all_to_all x2, blocking collectives, swap(): return lax.all_to_all(x, axes, split_axis=0, concat_axis=0, tiled=True)  41.7 us
    all_to_all x2, starting transfers between devices, swap(): return lax.all_to_all(x, axes, split_axis=0, concat_axis=0, tiled=True)  14.1 us
    all_gather x1, blocking collectives, step(): whole = lax.all_gather(part, CORE, axis=0, tiled=True)  6.38 us
    ppermute x2, waiting for transfers between devices, moved_rows(): return lax.ppermute(x, ROWS, pairs)  6.35 us
    all_to_all x2, waiting for transfers between devices, swap(): return lax.all_to_all(x, axes, split_axis=0, concat_axis=0, tiled=True)  3.68 us
    ppermute x1, starting transfers between devices, step(): other = lax.ppermute(terms[1], CORE, [(0, 1), (1, 0)])  3.15 us
    ppermute x2, starting transfers between devices, moved_rows(): return lax.ppermute(x, ROWS, pairs)  2.57 us
    pallas_call x1, Pallas kernels, step(): pl.pallas_call(send_body, grid=(1,), in_specs=[pl.BlockSpec(grad.shape, l...  1.91 us
  transfers between devices with their start and end apart: 5, of which 5 were waited for; matrix products, arithmetic and copies ran while one was open for 0% of the time, Pallas kernels for 2%

profile of v2, /device:TPU:1, one launch (start us, length us, event | category | flops | bytes accessed | tf_op | source)
XLA Modules:
  0.0 88.3 jit_solution(14367224502361468245)
XLA Ops:
  0.6 0.0 copy-start
  0.6 1.9 %shard_map.50 = (bf16[4,200,128]{2,1,0:T(8,128)(2,1)}, bf16[192,256]{1,0:T(8,128)(2,1)}) custom-call(bf16[192,512]{1,0:T(8,128)(2,1)} %bitcast.17, bf16[8,192,256]{2,1,0:T(8,128)(2,1)} %bitcast.12), custom_call_target="tpu_custom_call" | custom-call | flops 100000000 | bytes 500000 | tf_op jit(solution)/shard_map/pallas_call | solution.py:258
  2.6 10.2 %all-to-all-start = ((bf16[4,200,128]{2,1,0:T(8,128)(2,1)}), bf16[4,200,128]{2,1,0:T(8,128)(2,1)S(1)}, u32[]{:S(2)}, u32[]{:S(2)}) async-start(bf16[4,200,128]{2,1,0:T(8,128)(2,1)} %get-tuple-element.10), calls=%async_computation | async-start | bytes 409600 | tf_op jit(solution)/shard_map/all_to_all | solution.py:244
  12.7 1.3 %collective-permute-start = (bf16[192,256]{1,0:T(8,128)(2,1)}, bf16[192,256]{1,0:T(8,128)(2,1)S(1)}, u32[]{:S(2)}, u32[]{:S(2)}) collective-permute-start(bf16[192,256]{1,0:T(8,128)(2,1)} %get-tuple-element.11), channel_id=1, source_target_pairs={{0,4},{4,8},{8,12},{12,16},{16,20},{20,24},{24,28},{28,32},{32,36}... | collective-permute-start | bytes 294920 | tf_op jit(solution)/shard_map/ppermute | solution.py:240
  14.0 0.0 copy-done
  14.0 0.4 shard_map.51.split_ref
  14.4 2.3 %collective-permute-done.above_ref = bf16[192,256]{1,0:T(8,128)(2,1)S(1)} collective-permute-done((bf16[192,256]{1,0:T(8,128)(2,1)}, bf16[192,256]{1,0:T(8,128)(2,1)S(1)}, u32[]{:S(2)}, u32[]{:S(2)}) %collective-permute-start) | collective-permute-done | bytes 98336 | tf_op jit(solution)/shard_map/ppermute | solution.py:240
  16.7 1.7 %all-to-all-done.got_ref = bf16[4,200,128]{2,1,0:T(8,128)(2,1)S(1)} async-done(((bf16[4,200,128]{2,1,0:T(8,128)(2,1)}), bf16[4,200,128]{2,1,0:T(8,128)(2,1)S(1)}, u32[]{:S(2)}, u32[]{:S(2)}) %all-to-all-start) | async-done | bytes 204832 | tf_op jit(solution)/shard_map/all_to_all | solution.py:244
  18.4 1.0 %shard_map.52 = (f32[2,1536,128]{2,1,0:T(8,128)S(1)}, bf16[4,2,192,128]{3,2,1,0:T(8,128)(2,1)S(1)}) custom-call(bf16[4,200,128]{2,1,0:T(8,128)(2,1)S(1)} %all-to-all-done.got_ref, bf16[8,192,256]{2,1,0:T(8,128)(2,1)S(1)} %shard_map.51.split_ref, bf16[192,256]{1,0:T(8,128)(2,1)S(1)} %collective-permute-done.above_ref), custom_call_target="tpu_custom_call" | custom-call | flops 1000000000 | bytes 4000000 | tf_op jit(solution)/shard_map/pallas_call | solution.py:276
  19.4 0.1 slice_bitcast_fusion
  19.4 3.1 %collective-permute-start.1 = (f32[1536,128]{1,0:T(8,128)S(1)}, f32[1536,128]{1,0:T(8,128)S(1)}, u32[]{:S(2)}, u32[]{:S(2)}) collective-permute-start(f32[1536,128]{1,0:T(8,128)S(1)} %slice_bitcast_fusion), channel_id=1, source_target_pairs={{0,1},{1,0},{2,3},{3,2},{4,5},{5,4},{6,7},{7,6},{8,9},{9,8},{10,11... | collective-permute-start | bytes 2359304 | tf_op jit(solution)/shard_map/ppermute | solution.py:282
  22.6 1.9 %collective-permute-done.1.other_ref = f32[1536,128]{1,0:T(8,128)S(1)} collective-permute-done((f32[1536,128]{1,0:T(8,128)S(1)}, f32[1536,128]{1,0:T(8,128)S(1)}, u32[]{:S(2)}, u32[]{:S(2)}) %collective-permute-start.1) | collective-permute-done | bytes 786464 | tf_op jit(solution)/shard_map/ppermute | solution.py:282
  24.5 0.1 shard_map.53
  24.5 0.0 copy-start.1
  24.5 21.1 %all_to_all.20.in_ref = bf16[32,48,128]{2,1,0:T(8,128)(2,1)S(1)} all-to-all(bf16[32,48,128]{2,1,0:T(8,128)(2,1)S(1)} %bitcast.14), channel_id=1, replica_groups=mesh['r0'=2,'r1'=4,'z1'=8,'z0'=2,'c0'=2,'c1'=2] {'r0','r1','z0','c0'}, dimensions={0} | all-to-all | bytes 786432 | tf_op jit(solution)/shard_map/all_to_all | solution.py:244
  45.6 0.2 shard_map.54
  45.8 20.6 %all_to_all.21.in_ref = bf16[8,56,128]{2,1,0:T(8,128)(2,1)S(1)} all-to-all(bf16[8,56,128]{2,1,0:T(8,128)(2,1)S(1)} %shard_map.54), channel_id=1, replica_groups=mesh['r0'=2,'r1'=4,'z1'=8,'z0'=2,'c0'=2,'c1'=2] {'z1'}, dimensions={0} | all-to-all | bytes 229376 | tf_op jit(solution)/shard_map/all_to_all | solution.py:244
  66.5 1.1 %shard_map.55 = bf16[32,48,128]{2,1,0:T(8,128)(2,1)} custom-call(bf16[8,56,128]{2,1,0:T(8,128)(2,1)S(1)} %all_to_all.21.in_ref), custom_call_target="tpu_custom_call" | custom-call | flops 1000000 | bytes 1000000 | tf_op jit(solution)/shard_map/pallas_call | solution.py:289
  67.6 3.9 %all-to-all-start.3 = ((bf16[32,48,128]{2,1,0:T(8,128)(2,1)}), bf16[32,48,128]{2,1,0:T(8,128)(2,1)S(1)}, u32[]{:S(2)}, u32[]{:S(2)}) async-start(bf16[32,48,128]{2,1,0:T(8,128)(2,1)} %shard_map.55), calls=%async_computation.3 | async-start | bytes 786432 | tf_op jit(solution)/shard_map/all_to_all | solution.py:244
  71.5 1.3 %collective-permute-start.2 = (bf16[2,192,128]{2,1,0:T(8,128)(2,1)S(1)}, bf16[2,192,128]{2,1,0:T(8,128)(2,1)S(1)}, u32[]{:S(2)}, u32[]{:S(2)}) collective-permute-start(bf16[2,192,128]{2,1,0:T(8,128)(2,1)S(1)} %slice_bitcast_fusion.1), channel_id=1, source_target_pairs={{4,0},{8,4},{12,8},{16,12},{20,16},{24,20},{28,24},{32,28},{36,32}... | collective-permute-start | bytes 294920 | tf_op jit(solution)/shard_map/ppermute | solution.py:240
  72.8 4.1 %collective-permute-done.2.below_ref = bf16[2,192,128]{2,1,0:T(8,128)(2,1)S(1)} collective-permute-done((bf16[2,192,128]{2,1,0:T(8,128)(2,1)S(1)}, bf16[2,192,128]{2,1,0:T(8,128)(2,1)S(1)}, u32[]{:S(2)}, u32[]{:S(2)}) %collective-permute-start.2) | collective-permute-done | bytes 98336 | tf_op jit(solution)/shard_map/ppermute | solution.py:240
  76.8 0.0 copy-done.1
  76.8 1.8 %shard_map.56 = bf16[8,192,256]{2,1,0:T(8,128)(2,1)} custom-call(bf16[4,2,192,128]{3,2,1,0:T(8,128)(2,1)S(1)} %get-tuple-element.15.pair_ref, bf16[2,192,128]{2,1,0:T(8,128)(2,1)S(1)} %collective-permute-done.2.below_ref, bf16[3,3,192,192]{3,2,1,0:T(8,128)(2,1)S(1)} %copy-done.1), custom_call_target="tpu_custom_call" | custom-call | flops 1000000000 | bytes 2000000 | tf_op jit(solution)/shard_map/pallas_call | solution.py:291
  78.6 2.0 %all-to-all-done.3 = bf16[32,48,128]{2,1,0:T(8,128)(2,1)S(1)} async-done(((bf16[32,48,128]{2,1,0:T(8,128)(2,1)}), bf16[32,48,128]{2,1,0:T(8,128)(2,1)S(1)}, u32[]{:S(2)}, u32[]{:S(2)}) %all-to-all-start.3) | async-done | bytes 393248 | tf_op jit(solution)/shard_map/all_to_all | solution.py:244
  80.6 6.4 %all_gather.3.in_ref = bf16[3072,128]{1,0:T(8,128)(2,1)S(1)} all-gather(bf16[1536,128]{1,0:T(8,128)(2,1)S(1)} %bitcast.16), channel_id=1, replica_groups=mesh['r0'=2,'r1'=4,'z1'=8,'z0'=2,'c0'=2,'c1'=2] {'c1'}, dimensions={0}, use_global_device_ids=true | all-gather | bytes 1179648 | tf_op jit(solution)/shard_map/all_gather | solution.py:293
  87.0 1.4 %shard_map.57 = f32[9,192,192]{2,1,0:T(8,128)} custom-call(bf16[3072,128]{1,0:T(8,128)(2,1)S(1)} %all_gather.3.in_ref), custom_call_target="tpu_custom_call" | custom-call | flops 1000000 | bytes 2000000 | tf_op jit(solution)/shard_map/pallas_call | solution.py:294
  (1 shorter events, 0.0 us)
Async XLA Ops:
  0.6 13.4 %copy-start = (bf16[8,256,192]{1,2,0:T(8,128)(2,1)S(1)}, bf16[8,256,192]{1,2,0:T(8,128)(2,1)}, u32[]{:S(2)}) copy-start(bf16[8,256,192]{1,2,0:T(8,128)(2,1)} %param.4) | copy-start | bytes 2359300
  2.6 15.8 %all-to-all-start = ((bf16[4,200,128]{2,1,0:T(8,128)(2,1)}), bf16[4,200,128]{2,1,0:T(8,128)(2,1)S(1)}, u32[]{:S(2)}, u32[]{:S(2)}) async-start(bf16[4,200,128]{2,1,0:T(8,128)(2,1)} %get-tuple-element.10), calls=%async_computation | async-start | bytes 409600 | tf_op jit(solution)/shard_map/all_to_all | solution.py:244
  12.7 4.0 %collective-permute-start = (bf16[192,256]{1,0:T(8,128)(2,1)}, bf16[192,256]{1,0:T(8,128)(2,1)S(1)}, u32[]{:S(2)}, u32[]{:S(2)}) collective-permute-start(bf16[192,256]{1,0:T(8,128)(2,1)} %get-tuple-element.11), channel_id=1, source_target_pairs={{0,4},{4,8},{8,12},{12,16},{16,20},{20,24},{24,28},{28,32},{32,36}... | collective-permute-start | bytes 294920 | tf_op jit(solution)/shard_map/ppermute | solution.py:240
  19.4 5.0 %collective-permute-start.1 = (f32[1536,128]{1,0:T(8,128)S(1)}, f32[1536,128]{1,0:T(8,128)S(1)}, u32[]{:S(2)}, u32[]{:S(2)}) collective-permute-start(f32[1536,128]{1,0:T(8,128)S(1)} %slice_bitcast_fusion), channel_id=1, source_target_pairs={{0,1},{1,0},{2,3},{3,2},{4,5},{5,4},{6,7},{7,6},{8,9},{9,8},{10,11... | collective-permute-start | bytes 2359304 | tf_op jit(solution)/shard_map/ppermute | solution.py:282
  24.5 52.3 %copy-start.1 = (bf16[3,3,192,192]{3,2,1,0:T(8,128)(2,1)S(1)}, bf16[3,3,192,192]{3,2,1,0:T(8,128)(2,1)}, u32[]{:S(2)}) copy-start(bf16[3,3,192,192]{3,2,1,0:T(8,128)(2,1)} %weight_ref.1) | copy-start | bytes 1990660
  67.6 13.0 %all-to-all-start.3 = ((bf16[32,48,128]{2,1,0:T(8,128)(2,1)}), bf16[32,48,128]{2,1,0:T(8,128)(2,1)S(1)}, u32[]{:S(2)}, u32[]{:S(2)}) async-start(bf16[32,48,128]{2,1,0:T(8,128)(2,1)} %shard_map.55), calls=%async_computation.3 | async-start | bytes 786432 | tf_op jit(solution)/shard_map/all_to_all | solution.py:244
  71.5 5.4 %collective-permute-start.2 = (bf16[2,192,128]{2,1,0:T(8,128)(2,1)S(1)}, bf16[2,192,128]{2,1,0:T(8,128)(2,1)S(1)}, u32[]{:S(2)}, u32[]{:S(2)}) collective-permute-start(bf16[2,192,128]{2,1,0:T(8,128)(2,1)S(1)} %slice_bitcast_fusion.1), channel_id=1, source_target_pairs={{4,0},{8,4},{12,8},{16,12},{20,16},{24,20},{28,24},{32,28},{36,32}... | collective-permute-start | bytes 294920 | tf_op jit(solution)/shard_map/ppermute | solution.py:240

commit v3 on v2

--- a/solution.py
+++ b/solution.py
@@ -184,8 +184,53 @@
     out_ref[...] = jnp.broadcast_to(total.astype(BF)[None], out_ref.shape)
 
 
-def unpack_body(scale, in_ref, out_ref, whole, sem):
+def merge_matrix(width):
+    half = width // 2
+    n = lax.broadcasted_iota(jnp.int32, (width, width), 0)
+    q = lax.broadcasted_iota(jnp.int32, (width, width), 1)
+    return jnp.where(q == jnp.where(n < half, 2 * n, 2 * (n - half) + 1), 1.0, 0.0).astype(BF)
+
+
+def merged(even, odd, merge):
+    return mm(jnp.concatenate([even, odd], axis=1).astype(BF), merge, NN).astype(BF)
+
+
+def input_body(pair_ref, weight_ref, out_ref, part_ref):
+    rows, chans, width = out_ref.shape
+    half = rows // 2
+    grads = [pair_ref[k, 0] for k in range(half)]
+    moved = [pair_ref[k, 1] for k in range(half)]
+    here = jnp.concatenate(grads, axis=1)
+    right = jnp.concatenate(moved, axis=1)
+    here_down = jnp.concatenate(grads[1:], axis=1)
+    right_down = jnp.concatenate(moved[1:], axis=1)
+
+    def tap(a, b, g):
+        return mm(weight_ref[a, b], g, NN)
+
+    even_even = tap(1, 1, here)
+    even_odd = tap(1, 2, here) + tap(1, 0, right)
+    odd_even = tap(2, 1, here)
+    odd_odd = tap(2, 2, here) + tap(2, 0, right)
+    odd_even_down = tap(0, 1, here_down)
+    odd_odd_down = tap(0, 2, here_down) + tap(0, 0, right_down)
+    merge = merge_matrix(width)
+    for k in range(half):
+        cut = slice(k * LANES, (k + 1) * LANES)
+        out_ref[2 * k] = merged(even_even[:, cut], even_odd[:, cut], merge)
+        if k < half - 1:
+            out_ref[2 * k + 1] = merged(
+                odd_even[:, cut] + odd_even_down[:, cut], odd_odd[:, cut] + odd_odd_down[:, cut], merge
+            )
+        else:
+            part_ref[0] = odd_even[:, cut]
+            part_ref[1] = odd_odd[:, cut]
+            out_ref[2 * k + 1] = jnp.zeros((chans, width), BF)
+
+
+def last_body(scale, in_ref, below_ref, weight_ref, part_ref, _, out_ref, grad_ref, whole, line, sem):
     chans = out_ref.shape[-1]
+    rows, _, width = grad_ref.shape
     step = chans + chans // 2
     copies = []
     for t in range(9):
@@ -198,36 +243,17 @@
         copy = pltpu.make_async_copy(whole.at[t], out_ref.at[t], sem.at[t])
         copy.start()
         copies.append(copy)
+    block = below_ref[...]
+    here = block[:chans, :]
+    right = shifted([here], edges_of([block], chans))[0]
+    even = part_ref[0] + mm(weight_ref[0, 1], here, NN)
+    odd = part_ref[1] + mm(weight_ref[0, 2], here, NN) + mm(weight_ref[0, 0], right, NN)
+    line[...] = merged(even, odd, merge_matrix(width))
+    copy = pltpu.make_async_copy(line, grad_ref.at[rows - 1], sem.at[9])
+    copy.start()
+    copies.append(copy)
     for copy in copies:
         copy.wait()
-
-
-def input_body(pair_ref, below_ref, weight_ref, out_ref):
-    rows, _, width = out_ref.shape
-    half = rows // 2
-    grads = [pair_ref[k, 0] for k in range(half)] + [below_ref[0]]
-    moved = [pair_ref[k, 1] for k in range(half)] + [below_ref[1]]
-    here = jnp.concatenate(grads[:half], axis=1)
-    right = jnp.concatenate(moved[:half], axis=1)
-    here_down = jnp.concatenate(grads[1:], axis=1)
-    right_down = jnp.concatenate(moved[1:], axis=1)
-
-    def tap(a, b, g):
-        return mm(weight_ref[a, b], g, NN)
-
-    even_even = tap(1, 1, here)
-    even_odd = tap(1, 2, here) + tap(1, 0, right)
-    odd_even = tap(2, 1, here) + tap(0, 1, here_down)
-    odd_odd = tap(2, 2, here) + tap(2, 0, right) + tap(0, 2, here_down) + tap(0, 0, right_down)
-    q = lax.broadcasted_iota(jnp.int32, (width, width), 1)
-    n = lax.broadcasted_iota(jnp.int32, (width, width), 0)
-    target = jnp.where(n < LANES, 2 * n, 2 * (n - LANES) + 1)
-    merge = jnp.where(q == target, 1.0, 0.0).astype(BF)
-    for k in range(half):
-        cut = slice(k * LANES, (k + 1) * LANES)
-        for p, left, odd in ((2 * k, even_even, even_odd), (2 * k + 1, odd_even, odd_odd)):
-            both = jnp.concatenate([left[:, cut], odd[:, cut]], axis=1).astype(BF)
-            out_ref[p] = mm(both, merge, NN).astype(BF)
 
 
 def shape(dims, dtype):
@@ -273,6 +299,7 @@
     got = swap(sent, COLS)
     above = moved_rows(last, 1)
     split = call(split_body, shape((rows, chans, cols), BF), 2 * 10**8, 2 * 10**6)(lines)
+    below = moved_rows(got[0], -1)
     terms, pairs = call(
         filter_body,
         (shape((2, own, LANES), F32), shape((half, 2, chans, LANES), BF)),
@@ -280,25 +307,32 @@
         4 * 10**6,
     )(got, split, above)
     other = lax.ppermute(terms[1], CORE, [(0, 1), (1, 0)])
+    input_grad, odd_part = call(
+        input_body, (shape((rows, chans, cols), BF), shape((2, chans, LANES), F32)), 10**9, 2 * 10**6
+    )(pairs, weight)
     part = call(pair_body, shape((own, LANES), BF), 10**6, 2 * 10**6)(terms, other)
     part = swap(part.reshape(near, chunk, LANES), NEAR)
     part = call(near_body, shape((far, chunk + 8, LANES), BF), 10**6, 10**6)(part)
-    part, pairs = lax.optimization_barrier((part, pairs))
     part = swap(part, FAR)
-    below = moved_rows(pairs[0], -1)
     part = call(far_body, shape((near, chunk, LANES), BF), 10**6, 10**6)(part)
     part = swap(part, NEAR).reshape(own, LANES)
-    input_grad = call(input_body, shape((rows, chans, cols), BF), 10**9, 2 * 10**6)(pairs, below, weight)
-    part, input_grad = lax.optimization_barrier((part, input_grad))
     whole = lax.all_gather(part, CORE, axis=0, tiled=True)
-    filter_grad = pl.pallas_call(
-        functools.partial(unpack_body, 1.0 / math.sqrt(positions)),
-        out_shape=shape((9, chans, chans), F32),
-        out_specs=pl.BlockSpec(memory_space=pltpu.HBM),
-        scratch_shapes=[pltpu.VMEM((9, chans, chans), F32), pltpu.SemaphoreType.DMA((9,))],
+    stored = pl.BlockSpec(memory_space=pltpu.HBM)
+    local = pl.BlockSpec(memory_space=pltpu.VMEM)
+    filter_grad, input_grad = pl.pallas_call(
+        functools.partial(last_body, 1.0 / math.sqrt(positions)),
+        out_shape=(shape((9, chans, chans), F32), shape((rows, chans, cols), BF)),
+        in_specs=[local, local, local, local, stored],
+        out_specs=(stored, stored),
+        input_output_aliases={4: 1},
+        scratch_shapes=[
+            pltpu.VMEM((9, chans, chans), F32),
+            pltpu.VMEM((chans, cols), BF),
+            pltpu.SemaphoreType.DMA((10,)),
+        ],
         cost_estimate=pl.CostEstimate(flops=10**6, bytes_accessed=2 * 10**6, transcendentals=0),
         compiler_params=pltpu.CompilerParams(vmem_limit_bytes=24 * 1024 * 1024),
-    )(whole)
+    )(whole, below, weight, odd_part, input_grad)
     return (jnp.transpose(input_grad, (0, 2, 1)), filter_grad.reshape(3, 3, chans, chans))
 
 

time: 88.8 us -> 89 us (level)
    all_to_all x2, waiting for transfers between devices: 3.68 us -> 7.82 us  [swap(): return lax.all_to_all(x, axes, split_axis=0, concat_axis=0, tiled=True)]
    ppermute x2, waiting for transfers between devices: 6.35 us -> 2.29 us  [moved_rows(): return lax.ppermute(x, ROWS, pairs)]
  transfers between devices with their start and end apart: 5 -> 5, of which waited for: 5 -> 4; matrix products, arithmetic and copies ran while one was open for 0% -> 0% of each run, Pallas kernels for 2% -> 2%
where the time goes in v3:
time: 89 us; the launch traced here: 88.6 us
  blocking collectives  48.1 us (54%)
  starting transfers between devices  19.8 us (22%)
  waiting for transfers between devices  12 us (13%)
  Pallas kernels  7.93 us (9%)
    all_to_all x2, blocking collectives, swap(): return lax.all_to_all(x, axes, split_axis=0, concat_axis=0, tiled=True)  41.7 us
    all_to_all x2, starting transfers between devices, swap(): return lax.all_to_all(x, axes, split_axis=0, concat_axis=0, tiled=True)  14.1 us
    all_to_all x2, waiting for transfers between devices, swap(): return lax.all_to_all(x, axes, split_axis=0, concat_axis=0, tiled=True)  7.82 us
    all_gather x1, blocking collectives, step(): whole = lax.all_gather(part, CORE, axis=0, tiled=True)  6.38 us
    ppermute x1, starting transfers between devices, step(): other = lax.ppermute(terms[1], CORE, [(0, 1), (1, 0)])  3.15 us
    ppermute x2, starting transfers between devices, moved_rows(): return lax.ppermute(x, ROWS, pairs)  2.57 us
    ppermute x2, waiting for transfers between devices, moved_rows(): return lax.ppermute(x, ROWS, pairs)  2.29 us
    pallas_call x1, Pallas kernels, step(): pl.pallas_call(send_body, grid=(1,), in_specs=[pl.BlockSpec(grad.shape, l...  1.91 us
  transfers between devices with their start and end apart: 5, of which 4 were waited for; matrix products, arithmetic and copies ran while one was open for 0% of the time, Pallas kernels for 2%

profile of v3, /device:TPU:1, one launch (start us, length us, event | category | flops | bytes accessed | tf_op | source)
XLA Modules:
  0.0 88.6 jit_solution(3805474491000727632)
XLA Ops:
  0.6 0.0 copy-start
  0.6 1.9 %shard_map.50 = (bf16[4,200,128]{2,1,0:T(8,128)(2,1)}, bf16[192,256]{1,0:T(8,128)(2,1)}) custom-call(bf16[192,512]{1,0:T(8,128)(2,1)} %bitcast.17, bf16[8,192,256]{2,1,0:T(8,128)(2,1)} %bitcast.12), custom_call_target="tpu_custom_call" | custom-call | flops 100000000 | bytes 500000 | tf_op jit(solution)/shard_map/pallas_call | solution.py:284
  2.6 10.2 %all-to-all-start = ((bf16[4,200,128]{2,1,0:T(8,128)(2,1)}), bf16[4,200,128]{2,1,0:T(8,128)(2,1)S(1)}, u32[]{:S(2)}, u32[]{:S(2)}) async-start(bf16[4,200,128]{2,1,0:T(8,128)(2,1)} %get-tuple-element.10), calls=%async_computation | async-start | bytes 409600 | tf_op jit(solution)/shard_map/all_to_all | solution.py:270
  12.7 1.3 %collective-permute-start = (bf16[192,256]{1,0:T(8,128)(2,1)}, bf16[192,256]{1,0:T(8,128)(2,1)S(1)}, u32[]{:S(2)}, u32[]{:S(2)}) collective-permute-start(bf16[192,256]{1,0:T(8,128)(2,1)} %get-tuple-element.11), channel_id=1, source_target_pairs={{0,4},{4,8},{8,12},{12,16},{16,20},{20,24},{24,28},{28,32},{32,36}... | collective-permute-start | bytes 294920 | tf_op jit(solution)/shard_map/ppermute | solution.py:266
  14.0 0.0 copy-done
  14.0 0.4 shard_map.51.split_ref
  14.4 2.3 %collective-permute-done.above_ref = bf16[192,256]{1,0:T(8,128)(2,1)S(1)} collective-permute-done((bf16[192,256]{1,0:T(8,128)(2,1)}, bf16[192,256]{1,0:T(8,128)(2,1)S(1)}, u32[]{:S(2)}, u32[]{:S(2)}) %collective-permute-start) | collective-permute-done | bytes 98336 | tf_op jit(solution)/shard_map/ppermute | solution.py:266
  16.7 1.7 %all-to-all-done.got_ref = bf16[4,200,128]{2,1,0:T(8,128)(2,1)S(1)} async-done(((bf16[4,200,128]{2,1,0:T(8,128)(2,1)}), bf16[4,200,128]{2,1,0:T(8,128)(2,1)S(1)}, u32[]{:S(2)}, u32[]{:S(2)}) %all-to-all-start) | async-done | bytes 204832 | tf_op jit(solution)/shard_map/all_to_all | solution.py:270
  18.4 1.0 %shard_map.52 = (f32[2,1536,128]{2,1,0:T(8,128)S(1)}, bf16[4,2,192,128]{3,2,1,0:T(8,128)(2,1)S(1)}) custom-call(bf16[4,200,128]{2,1,0:T(8,128)(2,1)S(1)} %all-to-all-done.got_ref, bf16[8,192,256]{2,1,0:T(8,128)(2,1)S(1)} %shard_map.51.split_ref, bf16[192,256]{1,0:T(8,128)(2,1)S(1)} %collective-permute-done.above_ref), custom_call_target="tpu_custom_call" | custom-call | flops 1000000000 | bytes 4000000 | tf_op jit(solution)/shard_map/pallas_call | solution.py:303
  19.4 0.1 slice_bitcast_fusion
  19.4 3.1 %collective-permute-start.1 = (f32[1536,128]{1,0:T(8,128)S(1)}, f32[1536,128]{1,0:T(8,128)S(1)}, u32[]{:S(2)}, u32[]{:S(2)}) collective-permute-start(f32[1536,128]{1,0:T(8,128)S(1)} %slice_bitcast_fusion), channel_id=1, source_target_pairs={{0,1},{1,0},{2,3},{3,2},{4,5},{5,4},{6,7},{7,6},{8,9},{9,8},{10,11... | collective-permute-start | bytes 2359304 | tf_op jit(solution)/shard_map/ppermute | solution.py:309
  22.6 1.9 %collective-permute-done.1.other_ref = f32[1536,128]{1,0:T(8,128)S(1)} collective-permute-done((f32[1536,128]{1,0:T(8,128)S(1)}, f32[1536,128]{1,0:T(8,128)S(1)}, u32[]{:S(2)}, u32[]{:S(2)}) %collective-permute-start.1) | collective-permute-done | bytes 786464 | tf_op jit(solution)/shard_map/ppermute | solution.py:309
  24.5 0.1 shard_map.53
  24.5 0.0 copy-start.1
  24.5 21.1 %all_to_all.20.in_ref = bf16[32,48,128]{2,1,0:T(8,128)(2,1)S(1)} all-to-all(bf16[32,48,128]{2,1,0:T(8,128)(2,1)S(1)} %bitcast.14), channel_id=1, replica_groups=mesh['r0'=2,'r1'=4,'z1'=8,'z0'=2,'c0'=2,'c1'=2] {'r0','r1','z0','c0'}, dimensions={0} | all-to-all | bytes 786432 | tf_op jit(solution)/shard_map/all_to_all | solution.py:270
  45.6 0.2 shard_map.54
  45.8 20.6 %all_to_all.21.in_ref = bf16[8,56,128]{2,1,0:T(8,128)(2,1)S(1)} all-to-all(bf16[8,56,128]{2,1,0:T(8,128)(2,1)S(1)} %shard_map.54), channel_id=1, replica_groups=mesh['r0'=2,'r1'=4,'z1'=8,'z0'=2,'c0'=2,'c1'=2] {'z1'}, dimensions={0} | all-to-all | bytes 229376 | tf_op jit(solution)/shard_map/all_to_all | solution.py:270
  66.5 1.1 %shard_map.55 = bf16[32,48,128]{2,1,0:T(8,128)(2,1)} custom-call(bf16[8,56,128]{2,1,0:T(8,128)(2,1)S(1)} %all_to_all.21.in_ref), custom_call_target="tpu_custom_call" | custom-call | flops 1000000 | bytes 1000000 | tf_op jit(solution)/shard_map/pallas_call | solution.py:317
  67.5 3.9 %all-to-all-start.3 = ((bf16[32,48,128]{2,1,0:T(8,128)(2,1)}), bf16[32,48,128]{2,1,0:T(8,128)(2,1)S(1)}, u32[]{:S(2)}, u32[]{:S(2)}) async-start(bf16[32,48,128]{2,1,0:T(8,128)(2,1)} %shard_map.55), calls=%async_computation.3 | async-start | bytes 786432 | tf_op jit(solution)/shard_map/all_to_all | solution.py:270
  71.5 1.3 %collective-permute-start.2 = (bf16[200,128]{1,0:T(8,128)(2,1)S(1)}, bf16[200,128]{1,0:T(8,128)(2,1)S(1)}, u32[]{:S(2)}, u32[]{:S(2)}) collective-permute-start(bf16[200,128]{1,0:T(8,128)(2,1)S(1)} %slice_bitcast_fusion.1), channel_id=1, source_target_pairs={{4,0},{8,4},{12,8},{16,12},{20,16},{24,20},{28,24},{32,28},{36,32}... | collective-permute-start | bytes 153608 | tf_op jit(solution)/shard_map/ppermute | solution.py:266
  72.8 0.0 copy-done.1
  72.8 1.7 %shard_map.56 = (bf16[8,192,256]{2,1,0:T(8,128)(2,1)}, f32[2,192,128]{2,1,0:T(8,128)S(1)}) custom-call(bf16[4,2,192,128]{3,2,1,0:T(8,128)(2,1)S(1)} %get-tuple-element.13.pair_ref, bf16[3,3,192,192]{3,2,1,0:T(8,128)(2,1)S(1)} %copy-done.1), custom_call_target="tpu_custom_call" | custom-call | flops 1000000000 | bytes 2000000 | tf_op jit(solution)/shard_map/pallas_call | solution.py:310
  74.5 6.1 %all-to-all-done.3 = bf16[32,48,128]{2,1,0:T(8,128)(2,1)S(1)} async-done(((bf16[32,48,128]{2,1,0:T(8,128)(2,1)}), bf16[32,48,128]{2,1,0:T(8,128)(2,1)S(1)}, u32[]{:S(2)}, u32[]{:S(2)}) %all-to-all-start.3) | async-done | bytes 393248 | tf_op jit(solution)/shard_map/all_to_all | solution.py:270
  80.6 6.4 %all_gather.3.in_ref = bf16[3072,128]{1,0:T(8,128)(2,1)S(1)} all-gather(bf16[1536,128]{1,0:T(8,128)(2,1)S(1)} %bitcast.15), channel_id=1, replica_groups=mesh['r0'=2,'r1'=4,'z1'=8,'z0'=2,'c0'=2,'c1'=2] {'c1'}, dimensions={0}, use_global_device_ids=true | all-gather | bytes 1179648 | tf_op jit(solution)/shard_map/all_gather | solution.py:319
  87.0 0.0 collective-permute-done.2.below_ref
  87.0 1.6 %shard_map.57 = (f32[9,192,192]{2,1,0:T(8,128)}, bf16[8,192,256]{2,1,0:T(8,128)(2,1)}) custom-call(bf16[3072,128]{1,0:T(8,128)(2,1)S(1)} %all_gather.3.in_ref, bf16[200,128]{1,0:T(8,128)(2,1)S(1)} %collective-permute-done.2.below_ref, bf16[3,3,192,192]{3,2,1,0:T(8,128)(2,1)S(1)} %copy-done.1, ...), custom_call_target="tpu_custom_call", output_to_operand_aliasing={{1}: (4, {})} | custom-call | flops 1000000 | bytes 2000000 | tf_op jit(solution)/shard_map/pallas_call | solution.py:322
  (1 shorter events, 0.0 us)
Async XLA Ops:
  0.6 13.4 %copy-start = (bf16[8,256,192]{1,2,0:T(8,128)(2,1)S(1)}, bf16[8,256,192]{1,2,0:T(8,128)(2,1)}, u32[]{:S(2)}) copy-start(bf16[8,256,192]{1,2,0:T(8,128)(2,1)} %param.4) | copy-start | bytes 2359300
  2.6 15.8 %all-to-all-start = ((bf16[4,200,128]{2,1,0:T(8,128)(2,1)}), bf16[4,200,128]{2,1,0:T(8,128)(2,1)S(1)}, u32[]{:S(2)}, u32[]{:S(2)}) async-start(bf16[4,200,128]{2,1,0:T(8,128)(2,1)} %get-tuple-element.10), calls=%async_computation | async-start | bytes 409600 | tf_op jit(solution)/shard_map/all_to_all | solution.py:270
  12.7 4.0 %collective-permute-start = (bf16[192,256]{1,0:T(8,128)(2,1)}, bf16[192,256]{1,0:T(8,128)(2,1)S(1)}, u32[]{:S(2)}, u32[]{:S(2)}) collective-permute-start(bf16[192,256]{1,0:T(8,128)(2,1)} %get-tuple-element.11), channel_id=1, source_target_pairs={{0,4},{4,8},{8,12},{12,16},{16,20},{20,24},{24,28},{28,32},{32,36}... | collective-permute-start | bytes 294920 | tf_op jit(solution)/shard_map/ppermute | solution.py:266
  19.4 5.0 %collective-permute-start.1 = (f32[1536,128]{1,0:T(8,128)S(1)}, f32[1536,128]{1,0:T(8,128)S(1)}, u32[]{:S(2)}, u32[]{:S(2)}) collective-permute-start(f32[1536,128]{1,0:T(8,128)S(1)} %slice_bitcast_fusion), channel_id=1, source_target_pairs={{0,1},{1,0},{2,3},{3,2},{4,5},{5,4},{6,7},{7,6},{8,9},{9,8},{10,11... | collective-permute-start | bytes 2359304 | tf_op jit(solution)/shard_map/ppermute | solution.py:309
  24.5 48.2 %copy-start.1 = (bf16[3,3,192,192]{3,2,1,0:T(8,128)(2,1)S(1)}, bf16[3,3,192,192]{3,2,1,0:T(8,128)(2,1)}, u32[]{:S(2)}) copy-start(bf16[3,3,192,192]{3,2,1,0:T(8,128)(2,1)} %weight_ref.3) | copy-start | bytes 1990660
  67.5 13.0 %all-to-all-start.3 = ((bf16[32,48,128]{2,1,0:T(8,128)(2,1)}), bf16[32,48,128]{2,1,0:T(8,128)(2,1)S(1)}, u32[]{:S(2)}, u32[]{:S(2)}) async-start(bf16[32,48,128]{2,1,0:T(8,128)(2,1)} %shard_map.55), calls=%async_computation.3 | async-start | bytes 786432 | tf_op jit(solution)/shard_map/all_to_all | solution.py:270
  71.5 15.5 %collective-permute-start.2 = (bf16[200,128]{1,0:T(8,128)(2,1)S(1)}, bf16[200,128]{1,0:T(8,128)(2,1)S(1)}, u32[]{:S(2)}, u32[]{:S(2)}) collective-permute-start(bf16[200,128]{1,0:T(8,128)(2,1)S(1)} %slice_bitcast_fusion.1), channel_id=1, source_target_pairs={{4,0},{8,4},{12,8},{16,12},{20,16},{24,20},{28,24},{32,28},{36,32}... | collective-permute-start | bytes 153608 | tf_op jit(solution)/shard_map/ppermute | solution.py:266
